TPU v7x, 256 devices: a whole 4x4x8 slice. The times are simulated.
256 devices in a mesh: rows: 64 (over x_hi, z, y), cols: 4 (over x_lo, core).
Axes of the slice: x: 4 (x_hi: 2, x_lo: 2; x = x_hi * 2 + x_lo), y: 4, z: 8, core: 2. Of those that a mesh axis runs over, the one named last changes fastest.
Arguments:
- tokens: bfloat16 [768, 96, 768], P('rows', 'cols'), may hold values from -48 to 48
- ln_gain: float32 [768], replicated, may hold values from 0.5 to 1.5
- ln_bias: float32 [768], replicated, may hold values from -3 to 3
- qkv_weight: bfloat16 [768, 2304], replicated, may hold values from -3 to 3
- qkv_bias: float32 [2304], replicated, may hold values from -3 to 3
- rel_table: float32 [23, 23, 24], replicated, may hold values from -4 to 4
- proj_weight: bfloat16 [768, 768], replicated, may hold values from -0.21875 to 0.21875
- proj_bias: float32 [768], replicated, may hold values from -3 to 3
- branch_weight: bfloat16 [4, 768, 512], replicated, may hold values from -0.21875 to 0.21875
- branch_bias: float32 [4, 512], replicated, may hold values from -4 to 4
- join_block: bfloat16 [768, 512], replicated, may hold values from -0.109375 to 0.109375
- join_branch: bfloat16 [4, 512, 512], replicated, may hold values from -0.375 to 0.375
- bn_gain: float32 [512], replicated, may hold values from 0.25 to 1.75
- bn_bias: float32 [512], replicated, may hold values from -4 to 4
Outputs:
- joined: bfloat16 [768, 96, 512], P('rows', 'cols')
All inputs are finite; a program needn't handle non-finite values.
Results may differ from a plain program's by a relative error of at most 0.0049.
Values may be sent and summed in bfloat16 or wider, within the bound.
A program may use at most 128 MiB of HBM per device.

v0:
```python
import jax
import jax.numpy as jnp
import numpy as np
from jax import lax
from jax.sharding import PartitionSpec as P

WIN = 12
bin_scales = (1, 2, 3, 6)
bin_starts = (0, 1, 3, 6)
norm_eps = 1e-05
highest = lax.Precision.HIGHEST


def passed_along(value, axis, steps):
    count = lax.axis_size(axis)
    pairs = [(source, (source + steps) % count) for source in range(count)]
    return lax.ppermute(value, axis, pairs)


def layer_norm(values, norm_gain, norm_bias):
    floats = values.astype(jnp.float32)
    center = jnp.mean(floats, -1, keepdims=True)
    spread_sq = jnp.mean(jnp.square(floats - center), -1, keepdims=True)
    return ((floats - center) * lax.rsqrt(spread_sq + norm_eps) * norm_gain + norm_bias).astype(
        jnp.bfloat16
    )


def relative_bias(rel_table):
    steps_idx = jnp.arange(WIN, dtype=jnp.int32)
    offsets = steps_idx[:, None] - steps_idx[None, :] + WIN - 1
    onehot = (
        offsets[:, :, None] == jnp.arange(2 * WIN - 1, dtype=jnp.int32)[None, None, :]
    ).astype(jnp.float32)
    pair_bias = jnp.einsum("pra,qsb,abh->hpqrs", onehot, onehot, rel_table, precision=highest)
    return pair_bias.reshape(rel_table.shape[2], WIN * WIN, WIN * WIN)


def region_labels(positions, total):
    return (positions >= total - WIN).astype(jnp.int32) + (positions >= total - WIN // 2).astype(
        jnp.int32
    )


def window_mask(row_place, col_place, height, breadth):
    labels = (
        3 * region_labels(row_place, height)[:, None] + region_labels(col_place, breadth)[None, :]
    )
    labels = labels.reshape(row_place.shape[0] // WIN, WIN, col_place.shape[0] // WIN, WIN)
    labels = labels.transpose(0, 2, 1, 3).reshape(-1, WIN * WIN)
    return jnp.where(labels[:, :, None] != labels[:, None, :], -100.0, 0.0).astype(jnp.float32)


def window_attention(normed, qkv_weight, qkv_bias, proj_weight, proj_bias, pair_bias, mask_add):
    row_count, col_count, width = normed.shape
    heads_count = pair_bias.shape[0]
    head_size = width // heads_count
    windows = normed.reshape(row_count // WIN, WIN, col_count // WIN, WIN, width)
    windows = windows.transpose(0, 2, 1, 3, 4).reshape(-1, WIN * WIN, width)
    count_win = windows.shape[0]
    mixed = (
        jnp.dot(windows.reshape(-1, width), qkv_weight, preferred_element_type=jnp.float32)
        + qkv_bias
    )
    mixed = mixed.reshape(count_win, WIN * WIN, 3, heads_count, head_size)
    queries = (mixed[:, :, 0] * head_size ** (-0.5)).astype(jnp.bfloat16)
    keys_bf = mixed[:, :, 1].astype(jnp.bfloat16)
    values_bf = mixed[:, :, 2].astype(jnp.bfloat16)
    scores = jnp.einsum("wihd,wjhd->whij", queries, keys_bf, preferred_element_type=jnp.float32)
    scores = scores + pair_bias[None] + mask_add[:, None]
    weights = jax.nn.softmax(scores, axis=-1).astype(jnp.bfloat16)
    context = jnp.einsum("whij,wjhd->wihd", weights, values_bf, preferred_element_type=jnp.float32)
    context = context.astype(jnp.bfloat16).reshape(-1, width)
    output = jnp.dot(context, proj_weight, preferred_element_type=jnp.float32) + proj_bias
    output = output.reshape(row_count // WIN, col_count // WIN, WIN, WIN, width).transpose(
        0, 2, 1, 3, 4
    )
    return output.reshape(row_count, col_count, width)


def bin_tables(positions, total):
    pooling = []
    spread = []
    place_f = positions.astype(jnp.float32)
    for scale_value in bin_scales:
        levels = jnp.arange(scale_value, dtype=jnp.int32)
        pooling.append(
            (positions[:, None] // (total // scale_value) == levels[None, :]).astype(jnp.float32)
        )
        source = jnp.clip((place_f + 0.5) * (scale_value / total) - 0.5, 0.0, scale_value - 1.0)
        spread.append(
            jax.nn.relu(1.0 - jnp.abs(source[:, None] - levels[None, :].astype(jnp.float32)))
        )
    return (jnp.concatenate(pooling, 1), jnp.concatenate(spread, 1))


def cell_selectors():
    row_select = np.zeros((12, 50), np.float32)
    col_select = np.zeros((12, 50), np.float32)
    column = 0
    for scale_value, start_value in zip(bin_scales, bin_starts):
        for upper in range(scale_value):
            for lower in range(scale_value):
                row_select[start_value + upper, column] = 1.0
                col_select[start_value + lower, column] = 1.0
                column += 1
    return (jnp.asarray(row_select, jnp.float32), jnp.asarray(col_select, jnp.float32))


def cell_counts(height, breadth):
    sizes_list = []
    for scale_value in bin_scales:
        sizes_list += [float(height // scale_value * (breadth // scale_value))] * (
            scale_value * scale_value
        )
    return jnp.asarray(sizes_list, jnp.float32)[:, None]


def local_pools(values, row_table, col_table):
    by_rows = jnp.einsum(
        "rk,rcd->kcd",
        row_table.astype(values.dtype),
        values,
        preferred_element_type=jnp.float32,
        precision=highest,
    )
    pieces = []
    for scale_value, start_value in zip(bin_scales, bin_starts):
        cell_block = jnp.einsum(
            "acd,cb->abd",
            by_rows[start_value : start_value + scale_value],
            col_table[:, start_value : start_value + scale_value],
            precision=highest,
        )
        pieces.append(cell_block.reshape(scale_value * scale_value, -1))
    return jnp.concatenate(pieces, 0)


def branch_projections(pooled, branch_weight, branch_bias, join_branch):
    results = []
    start_row = 0
    for branch_index, scale_value in enumerate(bin_scales):
        cell_rows = pooled[start_row : start_row + scale_value * scale_value]
        hidden_map = jax.nn.relu(
            jnp.dot(cell_rows, branch_weight[branch_index].astype(jnp.float32), precision=highest)
            + branch_bias[branch_index]
        )
        results.append(
            jnp.dot(hidden_map, join_branch[branch_index].astype(jnp.float32), precision=highest)
        )
        start_row += scale_value * scale_value
    return jnp.concatenate(results, 0)


def spread_cells(projected, row_spread, col_spread):
    total_map = jnp.zeros(
        (row_spread.shape[0], col_spread.shape[0], projected.shape[1]), jnp.float32
    )
    start_row = 0
    for scale_value, start_value in zip(bin_scales, bin_starts):
        block_cells = projected[start_row : start_row + scale_value * scale_value].reshape(
            scale_value, scale_value, -1
        )
        across = jnp.einsum(
            "cb,abh->ach",
            col_spread[:, start_value : start_value + scale_value],
            block_cells,
            precision=highest,
        )
        total_map = total_map + jnp.einsum(
            "ra,ach->rch",
            row_spread[:, start_value : start_value + scale_value],
            across,
            precision=highest,
        )
        start_row += scale_value * scale_value
    return total_map


def shards(
    tokens,
    ln_gain,
    ln_bias,
    qkv_weight,
    qkv_bias,
    rel_table,
    proj_weight,
    proj_bias,
    branch_weight,
    branch_bias,
    join_block,
    join_branch,
    bn_gain,
    bn_bias,
):
    row_count, col_count, width = tokens.shape
    height = row_count * lax.axis_size("rows")
    breadth = col_count * lax.axis_size("cols")
    half = WIN // 2
    upper_rows = passed_along(tokens[:half], "rows", -1)
    rolled_tok = jnp.concatenate([tokens[half:], upper_rows], 0)
    left_cols = passed_along(rolled_tok[:, :half], "cols", -1)
    rolled_tok = jnp.concatenate([rolled_tok[:, half:], left_cols], 1)
    row_place = lax.axis_index("rows") * row_count + jnp.arange(row_count, dtype=jnp.int32)
    col_place = lax.axis_index("cols") * col_count + jnp.arange(col_count, dtype=jnp.int32)
    normed = layer_norm(rolled_tok, ln_gain, ln_bias)
    mask_add = window_mask(row_place, col_place, height, breadth)
    attended = window_attention(
        normed, qkv_weight, qkv_bias, proj_weight, proj_bias, relative_bias(rel_table), mask_add
    )
    block_out = (rolled_tok.astype(jnp.float32) + attended).astype(jnp.bfloat16)
    row_orig = (row_place + half) % height
    col_orig = (col_place + half) % breadth
    row_pool, row_spread = bin_tables(row_orig, height)
    col_pool, col_spread = bin_tables(col_orig, breadth)
    counts = cell_counts(height, breadth)
    everyone = float(height * breadth)
    direct = jnp.dot(
        block_out.reshape(-1, width), join_block, preferred_element_type=jnp.float32
    ).reshape(row_count, col_count, -1)
    local_cells = local_pools(block_out, row_pool, col_pool)
    local_weighted = local_pools(direct, row_spread, col_spread)
    pooled, weighted, direct_sum, direct_squares = lax.psum(
        (
            local_cells,
            local_weighted,
            jnp.sum(direct, axis=(0, 1)),
            jnp.sum(jnp.square(direct), axis=(0, 1)),
        ),
        ("rows", "cols"),
    )
    projected = branch_projections(pooled / counts, branch_weight, branch_bias, join_branch)
    pre_norm = direct + spread_cells(projected, row_spread, col_spread)
    row_select, col_select = cell_selectors()
    full_rows = bin_tables(jnp.arange(height, dtype=jnp.int32), height)[1]
    full_cols = bin_tables(jnp.arange(breadth, dtype=jnp.int32), breadth)[1]
    gram_rows = jnp.dot(full_rows.T, full_rows, precision=highest)
    gram_cols = jnp.dot(full_cols.T, full_cols, precision=highest)
    gram_cells = jnp.dot(
        row_select.T, jnp.dot(gram_rows, row_select, precision=highest), precision=highest
    )
    gram_cells = gram_cells * jnp.dot(
        col_select.T, jnp.dot(gram_cols, col_select, precision=highest), precision=highest
    )
    cell_mass = jnp.dot(jnp.sum(full_rows, 0), row_select, precision=highest) * jnp.dot(
        jnp.sum(full_cols, 0), col_select, precision=highest
    )
    lifted_sum = jnp.dot(cell_mass, projected, precision=highest)
    lifted_squares = jnp.sum(projected * jnp.dot(gram_cells, projected, precision=highest), 0)
    cross_terms = jnp.sum(projected * weighted, 0)
    mean_val = (direct_sum + lifted_sum) / everyone
    variance = (direct_squares + 2.0 * cross_terms + lifted_squares) / everyone - jnp.square(
        mean_val
    )
    joined = jax.nn.relu(
        (pre_norm - mean_val) * lax.rsqrt(variance + norm_eps) * bn_gain + bn_bias
    ).astype(jnp.bfloat16)
    tail_cols = passed_along(joined[:, col_count - half :], "cols", 1)
    joined = jnp.concatenate([tail_cols, joined[:, : col_count - half]], 1)
    tail_rows = passed_along(joined[row_count - half :], "rows", 1)
    joined = jnp.concatenate([tail_rows, joined[: row_count - half]], 0)
    return joined


def solution(mesh):
    in_specs = (
        P("rows", "cols", None),
        P(),
        P(),
        P(),
        P(),
        P(),
        P(),
        P(),
        P(),
        P(),
        P(),
        P(),
        P(),
        P(),
    )
    out_specs = P("rows", "cols", None)
    return jax.shard_map(shards, mesh=mesh, in_specs=in_specs, out_specs=out_specs, check_vma=False)
```

profile of v0, /device:TPU:4, one launch (start us, length us, event | category | flops | bytes accessed | tf_op | source)
XLA Modules:
  0.0 454.1 jit_solution(9545579387952552729)
XLA Ops:
  6.5 2.0 fusion.182
  8.5 8.2 %collective-permute-start = (bf16[6,24,768]{2,1,0:T(8,128)(2,1)}, bf16[6,24,768]{2,1,0:T(8,128)(2,1)}, u32[]{:S(2)}, u32[]{:S(2)}) collective-permute-start(bf16[6,24,768]{2,1,0:T(8,128)(2,1)} %get-tuple-element.14), channel_id=1, source_target_pairs={{0,252},{4,0},{8,4},{12,8},{16,12},{20,16},{24,20},{28,24},{32,28}... | collective-permute-start | bytes 663560 | tf_op jit(solution)/shard_map/ppermute | solution.py:17
  31.7 2.0 convolution_bitcast_fusion.1
  33.7 8.9 %convolution_bitcast_fusion = f32[24,12,12,12,12]{0,4,2,3,1:T(8,128)} fusion(f32[23,24,12,12,1]{1,3,0,2,4:T(8,128)S(1)} %convolution_bitcast_fusion.1, s32[12,12]{1,0:T(8,128)S(1)} %subtract_add_fusion), kind=kOutput, calls=%fused_computation.1 | convolution fusion | flops 137358576 | bytes 2309184 | tf_op jit(solution)/shard_map/pra,qsb,abh->hpqrs/dot_general | solution.py:35
  42.6 12.3 %copy.59 = f32[24,12,12,12,12]{0,4,3,2,1:T(8,128)} copy(f32[24,12,12,12,12]{0,4,2,3,1:T(8,128)} %convolution_bitcast_fusion) | data formatting | bytes 3981312 | tf_op jit(solution)/shard_map/pra,qsb,abh->hpqrs/transpose | solution.py:35
  54.9 13.0 %add.642 = f32[24,144,144]{0,2,1:T(8,128)} reshape(f32[24,12,12,12,12]{0,4,3,2,1:T(8,128)} %copy.59) | data formatting | bytes 3981312 | tf_op jit(solution)/shard_map/add | solution.py:70
  67.9 12.6 %copy.60 = f32[24,144,144]{1,2,0:T(8,128)} copy(f32[24,144,144]{0,2,1:T(8,128)} %add.642) | data formatting | bytes 3981312 | tf_op jit(solution)/shard_map/add | solution.py:70
  104.4 2.1 fusion.181
  106.5 2.3 reshape.627
  111.2 1.9 reshape_reshape.3
  113.2 3.7 convolution_add_fusion
  116.9 2.4 copy.54
  119.3 5.1 %reshape.609 = f32[2,144,3,24,32]{1,0,4,3,2:T(2,128)} reshape(f32[288,2304]{0,1:T(8,128)S(1)} %copy.54) | data formatting | bytes 5308416 | tf_op jit(solution)/shard_map/reshape | solution.py:65
  124.4 2.8 copy.144
  128.9 4.0 fusion.18
  132.9 10.7 %fusion.184 = (f32[2,24,144]{2,1,0:T(8,128)S(1)}, f32[2,24,144,144]{2,3,1,0:T(8,128)}) fusion(f32[2,24,144,144]{2,3,1,0:T(8,128)} %fusion.18, f32[2,144,144]{1,2,0:T(8,128)S(1)} %copy-done.10, f32[24,144,144]{1,2,0:T(8,128)S(1)} %copy-done.3), kind=kOutput, calls=%fused_computation.308 | output fusion | flops 5972111 | bytes 10146816 | tf_op jit(solution)/shard_map/sub | solution.py:71
  143.6 3.7 fusion.8
  148.6 1.8 convolution_add_fusion.1
  153.1 2.2 multiply_reduce_fusion.1
  170.6 74.0 %all-reduce = (f32[512]{0:T(512)}, f32[512]{0:T(512)}) all-reduce(f32[512]{0:T(512)} %get-tuple-element.6, f32[512]{0:T(512)} %get-tuple-element.5), channel_id=1, replica_groups=mesh['rows'=64,'cols'=4] {'rows','cols'}, use_global_device_ids=true, to_apply=%region_6.7 | all-reduce | flops 1024 | bytes 8192 | tf_op jit(solution)/shard_map/psum | solution.py:223
  244.6 167.0 %all-reduce.4.cloned.1.call-done = (f32[50,768]{1,0:T(8,128)}, f32[50,512]{1,0:T(8,128)}) async-done(((f32[50,768]{1,0:T(8,128)}, f32[50,512]{1,0:T(8,128)}), (f32[50,768]{1,0:T(8,128)}, f32[50,512]{1,0:T(8,128)})) %all-reduce.4.cloned.1.call-update) | async-done | bytes 256016 | tf_op jit(solution)/shard_map/psum | solution.py:223
  429.2 2.2 fusion.40
  431.5 4.0 collective-permute-done.2
  435.7 10.8 %collective-permute-done.3 = bf16[6,24,512]{2,1,0:T(8,128)(2,1)S(1)} collective-permute-done((bf16[6,24,512]{2,1,0:T(8,128)(2,1)S(1)}, bf16[6,24,512]{2,1,0:T(8,128)(2,1)S(1)}, u32[]{:S(2)}, u32[]{:S(2)}) %collective-permute-start.3) | collective-permute-done | bytes 147488 | tf_op jit(solution)/shard_map/ppermute | solution.py:17
  (210 shorter events, 80.1 us)
Async XLA Ops:
  6.5 106.7 %copy-start = (bf16[768,2304]{1,0:T(8,128)(2,1)S(1)}, bf16[768,2304]{1,0:T(8,128)(2,1)}, u32[]{:S(2)}) copy-start(bf16[768,2304]{1,0:T(8,128)(2,1)} %param.20) | copy-start | bytes 10616836
  6.5 405.0 %all-reduce.4.cloned.1.call-start = ((), (), s32[]{:S(2)}) async-start(), calls=%async_computation | async-start | bytes 573440 | tf_op jit(solution)/shard_map/psum | solution.py:223
  8.5 87.3 %collective-permute-start = (bf16[6,24,768]{2,1,0:T(8,128)(2,1)}, bf16[6,24,768]{2,1,0:T(8,128)(2,1)}, u32[]{:S(2)}, u32[]{:S(2)}) collective-permute-start(bf16[6,24,768]{2,1,0:T(8,128)(2,1)} %get-tuple-element.14), channel_id=1, source_target_pairs={{0,252},{4,0},{8,4},{12,8},{16,12},{20,16},{24,20},{28,24},{32,28}... | collective-permute-start | bytes 663560 | tf_op jit(solution)/shard_map/ppermute | solution.py:17
  17.9 10.8 %copy-start.17 = (f32[6]{0:T(128)}, f32[6]{0:T(128)S(1)}, u32[]{:S(2)}) copy-start(f32[6]{0:T(128)S(1)} %iota_convert_fusion) | copy-start | bytes 76
  17.9 24.7 %copy-start.19 = (f32[3]{0:T(128)}, f32[3]{0:T(128)S(1)}, u32[]{:S(2)}) copy-start(f32[3]{0:T(128)S(1)} %iota_convert_fusion.1) | copy-start | bytes 40
  67.9 22.5 %copy-start.13 = (f32[12,50]{1,0:T(8,128)S(1)}, f32[12,50]{1,0:T(8,128)}, u32[]{:S(2)}) copy-start(f32[12,50]{1,0:T(8,128)} %constant.264.clone) | copy-start | bytes 7204
  67.9 25.8 %copy-start.12 = (f32[12,50]{1,0:T(8,128)S(1)}, f32[12,50]{1,0:T(8,128)}, u32[]{:S(2)}) copy-start(f32[12,50]{1,0:T(8,128)} %constant.265.clone) | copy-start | bytes 7204
  88.9 7.9 %copy-start.14 = (f32[96,6]{0,1:T(8,128)}, f32[96,6]{0,1:T(8,128)S(1)}, u32[]{:S(2)}) copy-start(f32[96,6]{0,1:T(8,128)S(1)} %subtract_maximum_fusion.3) | copy-start | bytes 6916
  89.6 7.1 %copy-start.21 = (f32[96,3]{0,1:T(4,128)}, f32[96,3]{0,1:T(4,128)S(1)}, u32[]{:S(2)}) copy-start(f32[96,3]{0,1:T(4,128)S(1)} %subtract_maximum_fusion.9) | copy-start | bytes 3460
  90.3 6.4 %copy-start.24 = (f32[96,2]{0,1:T(2,128)}, f32[96,2]{0,1:T(2,128)S(1)}, u32[]{:S(2)}) copy-start(f32[96,2]{0,1:T(2,128)S(1)} %subtract_maximum_fusion.14) | copy-start | bytes 2308
  96.8 4.2 collective-permute-start.1
  158.2 10.8 %copy-start.15 = (f32[96,6]{0,1:T(8,128)S(1)}, f32[96,6]{0,1:T(8,128)}, u32[]{:S(2)}) copy-start(f32[96,6]{0,1:T(8,128)} %copy-done.14) | copy-start | bytes 6916
  160.2 257.2 %copy-start.9 = (bf16[4,512,512]{2,1,0:T(8,128)(2,1)S(1)}, bf16[4,512,512]{2,1,0:T(8,128)(2,1)}, u32[]{:S(2)}) copy-start(bf16[4,512,512]{2,1,0:T(8,128)(2,1)} %param.28) | copy-start | bytes 6291460
  163.9 254.1 %copy-start.26 = (f32[1,512]{1,0:T(1,128)S(1)}, f32[1,512]{1,0:T(1,128)}, u32[]{:S(2)}) copy-start(f32[1,512]{1,0:T(1,128)} %get-tuple-element.15) | copy-start | bytes 6148
  412.5 8.6 %copy-start.11 = (f32[50,512]{1,0:T(8,128)S(1)}, f32[50,512]{1,0:T(8,128)}, u32[]{:S(2)}) copy-start(f32[50,512]{1,0:T(8,128)} %get-tuple-element.10) | copy-start | bytes 307204
  412.6 8.6 %copy-start.16 = (f32[50,50]{1,0:T(8,128)S(1)}, f32[50,50]{1,0:T(8,128)}, u32[]{:S(2)}) copy-start(f32[50,50]{1,0:T(8,128)} %convolution_multiply_fusion.1) | copy-start | bytes 30004
  414.1 7.4 %copy-start.33 = (f32[24]{0:T(128)S(1)}, f32[24]{0:T(128)}, u32[]{:S(2)}) copy-start(f32[24]{0:T(128)} %get-tuple-element.23) | copy-start | bytes 292
  414.1 7.9 %copy-start.34 = (f32[12]{0:T(128)S(1)}, f32[12]{0:T(128)}, u32[]{:S(2)}) copy-start(f32[12]{0:T(128)} %get-tuple-element.27) | copy-start | bytes 148
  415.8 7.3 %copy-start.20 = (f32[3]{0:T(128)S(1)}, f32[3]{0:T(128)}, u32[]{:S(2)}) copy-start(f32[3]{0:T(128)} %copy-done.19) | copy-start | bytes 40
  415.8 7.3 %copy-start.31 = (f32[24]{0:T(128)S(1)}, f32[24]{0:T(128)}, u32[]{:S(2)}) copy-start(f32[24]{0:T(128)} %get-tuple-element.24) | copy-start | bytes 292
  417.8 7.4 %copy-start.23 = (f32[2]{0:T(128)S(1)}, f32[2]{0:T(128)}, u32[]{:S(2)}) copy-start(f32[2]{0:T(128)} %iota_convert_fusion.2) | copy-start | bytes 28
  423.5 23.8 %copy-start.1 = (bf16[768,2304]{1,0:T(8,128)(2,1)S(1)}, bf16[768,2304]{1,0:T(8,128)(2,1)}, u32[]{:S(2)}) copy-start(bf16[768,2304]{1,0:T(8,128)(2,1)} %param.20) | copy-start | bytes 10616836
  431.4 4.1 collective-permute-start.2
  435.6 10.9 %collective-permute-start.3 = (bf16[6,24,512]{2,1,0:T(8,128)(2,1)S(1)}, bf16[6,24,512]{2,1,0:T(8,128)(2,1)S(1)}, u32[]{:S(2)}, u32[]{:S(2)}) collective-permute-start(bf16[6,24,512]{2,1,0:T(8,128)(2,1)S(1)} %fusion.65), channel_id=1, source_target_pairs={{0,4},{4,8},{8,12},{12,16},{16,20},{20,24},{24,28},{28,32},{32,36}... | collective-permute-start | bytes 442376 | tf_op jit(solution)/shard_map/ppermute | solution.py:17
  (22 other events, 89.5 us)
Sparse Core Ops, SparseCore 0:
  168.5 242.9 all-reduce.3
where the time goes:
time: 456 us; the launch traced here: 454 us
  waiting for transfers between devices  183 us (40%)
  blocking collectives  74 us (16%)
  local copies, waits for them, and re-layouts  67.4 us (15%)
  matrix products  54.9 us (12%)
  other arithmetic  50.5 us (11%)
  between operations  14.1 us (3%)
  starting transfers between devices  9.95 us (2%)
    psum x1, waiting for transfers between devices, shards(): lax.psum((local_cells, local_weighted, jnp.sum(direct, axis=(0, 1)), jnp....  167 us
    psum x1, blocking collectives, shards(): lax.psum((local_cells, local_weighted, jnp.sum(direct, axis=(0, 1)), jnp....  74 us
    add x2, local copies, waits for them, and re-layouts, window_attention(): scores = scores + pair_bias[None] + mask_add[:, None]  25.6 us
    ppermute x4, waiting for transfers between devices, passed_along(): return lax.ppermute(value, axis, pairs)  16.4 us
    transpose x1, local copies, waits for them, and re-layouts, relative_bias(): jnp.einsum('pra,qsb,abh->hpqrs', onehot, onehot, rel_table, precision=hig...  12.3 us
    dot_general x2, matrix products, relative_bias(): jnp.einsum('pra,qsb,abh->hpqrs', onehot, onehot, rel_table, precision=hig...  10.9 us
    sub x1, other arithmetic, window_attention(): weights = jax.nn.softmax(scores, axis=-1).astype(jnp.bfloat16)  10.7 us
    ppermute x4, starting transfers between devices, passed_along(): return lax.ppermute(value, axis, pairs)  9.95 us
  transfers between devices with their start and end apart: 5, of which 4 were waited for; matrix products, arithmetic and copies ran while one was open for 18% of the time, Pallas kernels for 0%

commit v1 on v0

--- a/solution.py
+++ b/solution.py
@@ -221,13 +221,16 @@
     local_cells = local_pools(block_out, row_pool, col_pool)
     local_weighted = local_pools(direct, row_spread, col_spread)
     pooled, weighted, direct_sum, direct_squares = lax.psum(
-        (
-            local_cells,
-            local_weighted,
-            jnp.sum(direct, axis=(0, 1)),
-            jnp.sum(jnp.square(direct), axis=(0, 1)),
+        lax.psum(
+            (
+                local_cells,
+                local_weighted,
+                jnp.sum(direct, axis=(0, 1)),
+                jnp.sum(jnp.square(direct), axis=(0, 1)),
+            ),
+            "rows",
         ),
-        ("rows", "cols"),
+        "cols",
     )
     projected = branch_projections(pooled / counts, branch_weight, branch_bias, join_branch)
     pre_norm = direct + spread_cells(projected, row_spread, col_spread)

time: 456 us -> 1040 us (2.28)
  waiting for transfers between devices: 183 us -> 659 us
  blocking collectives: 74 us -> 188 us
    psum x1, waiting for transfers between devices: 167 us -> 643 us  [shards(): lax.psum((local_cells, local_weighted, jnp.sum(direct, axis=(0, 1)), jnp....]
    psum x1, blocking collectives: 74 us -> 181 us  [shards(): lax.psum((local_cells, local_weighted, jnp.sum(direct, axis=(0, 1)), jnp....]
  transfers between devices with their start and end apart: 5 -> 6, of which waited for: 4 -> 4; matrix products, arithmetic and copies ran while one was open for 18% -> 8% of each run, Pallas kernels for 0% -> 0%
where the time goes in v1:
time: 1040 us
  waiting for transfers between devices  659 us (63%)
  blocking collectives  188 us (18%)
  local copies, waits for them, and re-layouts  67.4 us (6%)
  matrix products  56.8 us (5%)
  other arithmetic  47 us (5%)
  between operations  14.1 us (1%)
    psum x1, waiting for transfers between devices, shards(): lax.psum((local_cells, local_weighted, jnp.sum(direct, axis=(0, 1)), jnp....  643 us
    psum x1, blocking collectives, shards(): lax.psum((local_cells, local_weighted, jnp.sum(direct, axis=(0, 1)), jnp....  181 us
    add x2, local copies, waits for them, and re-layouts, window_attention(): scores = scores + pair_bias[None] + mask_add[:, None]  25.6 us
  transfers between devices with their start and end apart: 6, of which 4 were waited for; matrix products, arithmetic and copies ran while one was open for 8% of the time, Pallas kernels for 0%

profile of v1, /device:TPU:4, one launch (start us, length us, event | category | flops | bytes accessed | tf_op | source)
XLA Modules:
  0.0 1042.5 jit_solution(9720862387976954578)
XLA Ops:
  6.5 2.0 fusion.182
  8.5 8.2 collective-permute-start
  31.3 2.0 convolution_bitcast_fusion.1
  33.3 8.9 convolution_bitcast_fusion
  42.2 12.3 %copy.59 = f32[24,12,12,12,12]{0,4,3,2,1:T(8,128)} copy(f32[24,12,12,12,12]{0,4,2,3,1:T(8,128)} %convolution_bitcast_fusion) | data formatting | bytes 3981312 | tf_op jit(solution)/shard_map/pra,qsb,abh->hpqrs/transpose | solution.py:35
  54.5 13.0 %add.650 = f32[24,144,144]{0,2,1:T(8,128)} reshape(f32[24,12,12,12,12]{0,4,3,2,1:T(8,128)} %copy.59) | data formatting | bytes 3981312 | tf_op jit(solution)/shard_map/add | solution.py:70
  67.5 12.6 %copy.60 = f32[24,144,144]{1,2,0:T(8,128)} copy(f32[24,144,144]{0,2,1:T(8,128)} %add.650) | data formatting | bytes 3981312 | tf_op jit(solution)/shard_map/add | solution.py:70
  102.6 2.1 fusion.181
  104.7 2.3 reshape.627
  109.4 1.9 reshape_reshape.3
  111.4 3.7 convolution_add_fusion
  115.1 2.4 copy.54
  117.5 5.1 reshape.609
  122.6 2.8 copy.144
  127.1 4.0 fusion.18
  131.1 10.7 %fusion.184 = (f32[2,24,144]{2,1,0:T(8,128)S(1)}, f32[2,24,144,144]{2,3,1,0:T(8,128)}) fusion(f32[2,24,144,144]{2,3,1,0:T(8,128)} %fusion.18, f32[2,144,144]{1,2,0:T(8,128)S(1)} %copy-done.10, f32[24,144,144]{1,2,0:T(8,128)S(1)} %copy-done.3), kind=kOutput, calls=%fused_computation.308 | output fusion | flops 5972111 | bytes 10146816 | tf_op jit(solution)/shard_map/sub | solution.py:71
  141.8 3.8 fusion.8
  151.3 2.1 multiply_reduce_fusion.1
  168.2 642.7 %all-reduce.7.cloned.1.call-done = (f32[50,768]{1,0:T(8,128)}, f32[50,512]{1,0:T(8,128)}) async-done(((f32[50,768]{1,0:T(8,128)}, f32[50,512]{1,0:T(8,128)}), (f32[50,768]{1,0:T(8,128)}, f32[50,512]{1,0:T(8,128)})) %all-reduce.7.cloned.1.call-update) | async-done | bytes 256016 | tf_op jit(solution)/shard_map/psum | solution.py:224
  812.5 181.1 %all-reduce = (f32[512]{0:T(512)S(1)}, f32[512]{0:T(512)S(1)}) all-reduce(f32[512]{0:T(512)} %get-tuple-element.6, f32[512]{0:T(512)} %get-tuple-element.5), channel_id=1, replica_groups=mesh['rows'=64,'cols'=4] {'rows'}, use_global_device_ids=true, to_apply=%region_7.8 | all-reduce | flops 1024 | bytes 8192 | tf_op jit(solution)/shard_map/psum | solution.py:224
  993.6 6.4 all-reduce.2
  1017.1 2.2 fusion.40
  1019.5 4.0 collective-permute-done.2
  1023.6 11.2 %collective-permute-done.3 = bf16[6,24,512]{2,1,0:T(8,128)(2,1)S(1)} collective-permute-done((bf16[6,24,512]{2,1,0:T(8,128)(2,1)S(1)}, bf16[6,24,512]{2,1,0:T(8,128)(2,1)S(1)}, u32[]{:S(2)}, u32[]{:S(2)}) %collective-permute-start.3) | collective-permute-done | bytes 147488 | tf_op jit(solution)/shard_map/ppermute | solution.py:17
  (212 shorter events, 80.5 us)
Async XLA Ops:
  6.5 104.8 %copy-start = (bf16[768,2304]{1,0:T(8,128)(2,1)S(1)}, bf16[768,2304]{1,0:T(8,128)(2,1)}, u32[]{:S(2)}) copy-start(bf16[768,2304]{1,0:T(8,128)(2,1)} %param.20) | copy-start | bytes 10616836
  6.5 804.4 %all-reduce.7.cloned.1.call-start = ((), (), s32[]{:S(2)}) async-start(), calls=%async_computation | async-start | bytes 573440 | tf_op jit(solution)/shard_map/psum | solution.py:224
  8.5 85.5 %collective-permute-start = (bf16[6,24,768]{2,1,0:T(8,128)(2,1)}, bf16[6,24,768]{2,1,0:T(8,128)(2,1)}, u32[]{:S(2)}, u32[]{:S(2)}) collective-permute-start(bf16[6,24,768]{2,1,0:T(8,128)(2,1)} %get-tuple-element.18), channel_id=1, source_target_pairs={{0,252},{4,0},{8,4},{12,8},{16,12},{20,16},{24,20},{28,24},{32,28}... | collective-permute-start | bytes 663560 | tf_op jit(solution)/shard_map/ppermute | solution.py:17
  18.0 10.3 copy-start.15
  18.0 24.2 %copy-start.18 = (f32[3]{0:T(128)}, f32[3]{0:T(128)S(1)}, u32[]{:S(2)}) copy-start(f32[3]{0:T(128)S(1)} %iota_convert_fusion.1) | copy-start | bytes 40
  67.5 20.3 %copy-start.13 = (f32[12,50]{1,0:T(8,128)S(1)}, f32[12,50]{1,0:T(8,128)}, u32[]{:S(2)}) copy-start(f32[12,50]{1,0:T(8,128)} %constant.264.clone) | copy-start | bytes 7204
  67.5 22.5 %copy-start.12 = (f32[12,50]{1,0:T(8,128)S(1)}, f32[12,50]{1,0:T(8,128)}, u32[]{:S(2)}) copy-start(f32[12,50]{1,0:T(8,128)} %constant.265.clone) | copy-start | bytes 7204
  95.0 4.2 collective-permute-start.1
  156.4 10.9 %copy-start.14 = (f32[12,50]{1,0:T(8,128)S(1)}, f32[12,50]{1,0:T(8,128)}, u32[]{:S(2)}) copy-start(f32[12,50]{1,0:T(8,128)} %constant.264.clone) | copy-start | bytes 7204
  158.4 847.5 %copy-start.9 = (bf16[4,512,512]{2,1,0:T(8,128)(2,1)S(1)}, bf16[4,512,512]{2,1,0:T(8,128)(2,1)}, u32[]{:S(2)}) copy-start(bf16[4,512,512]{2,1,0:T(8,128)(2,1)} %param.28) | copy-start | bytes 6291460
  162.2 844.4 %copy-start.23 = (f32[1,512]{1,0:T(1,128)S(1)}, f32[1,512]{1,0:T(1,128)}, u32[]{:S(2)}) copy-start(f32[1,512]{1,0:T(1,128)} %get-tuple-element.19) | copy-start | bytes 6148
  166.6 833.5 %all-reduce.9.cloned.1.call-start = ((), (), s32[]{:S(2)}) async-start(), calls=%async_computation.1 | async-start | bytes 573440 | tf_op jit(solution)/shard_map/psum | solution.py:223
  1001.1 8.4 copy-start.38
  1001.1 8.6 copy-start.11
  1002.7 7.4 copy-start.17
  1002.7 7.4 copy-start.30
  1002.7 7.9 copy-start.31
  1004.3 7.3 copy-start.19
  1004.4 7.3 copy-start.28
  1006.3 7.5 copy-start.21
  1006.3 8.4 copy-start.32
  1012.1 23.6 %copy-start.1 = (bf16[768,2304]{1,0:T(8,128)(2,1)S(1)}, bf16[768,2304]{1,0:T(8,128)(2,1)}, u32[]{:S(2)}) copy-start(bf16[768,2304]{1,0:T(8,128)(2,1)} %param.20) | copy-start | bytes 10616836
  1019.3 4.1 collective-permute-start.2
  1023.5 11.3 %collective-permute-start.3 = (bf16[6,24,512]{2,1,0:T(8,128)(2,1)S(1)}, bf16[6,24,512]{2,1,0:T(8,128)(2,1)S(1)}, u32[]{:S(2)}, u32[]{:S(2)}) collective-permute-start(bf16[6,24,512]{2,1,0:T(8,128)(2,1)S(1)} %fusion.65), channel_id=1, source_target_pairs={{0,4},{4,8},{8,12},{12,16},{16,20},{20,24},{24,28},{28,32},{32,36}... | collective-permute-start | bytes 442376 | tf_op jit(solution)/shard_map/ppermute | solution.py:17
  (22 other events, 89.4 us)
Sparse Core Ops, SparseCore 0:
  166.7 644.1 all-reduce.6
  813.7 38.8 all-reduce.8
